TPU v7x, 32 devices: a whole 2x2x4 slice. The times are simulated.
32 devices in a mesh: dp: 8 (over z, x), expert: 4 (over y, core).
Axes of the slice: x: 2, y: 2, z: 4, core: 2. Of those that a mesh axis runs over, the one named last changes fastest.
Arguments:
- queries: bfloat16 [256, 2048], P(('dp', 'expert')), may hold values from -8 to 8
- fresh_key: bfloat16 [256, 256], P(('dp', 'expert')), may hold values from -4 to 4
- fresh_value: bfloat16 [256, 256], P(('dp', 'expert')), may hold values from -4 to 4
- cached_keys: bfloat16 [256, 128, 256], P(('dp', 'expert')), may hold values from -8 to 8
- cached_values: bfloat16 [256, 128, 256], P(('dp', 'expert')), may hold values from -4 to 4
- lengths: int32 [256], P(('dp', 'expert')), may hold values from 2 to 128
- sink_logit_rows: float32 [32], replicated, may hold values from 1 to 5
- residual: bfloat16 [256, 2880], P('dp', 'expert'), may hold values from -6 to 6
- o_weight: bfloat16 [2880, 2048], P('expert'), may hold values from -0.125 to 0.125
- norm_gain: float32 [2880], replicated, may hold values from 0.5 to 1.5
- expert_ids: int32 [256, 4], replicated, may hold values from 0 to 7, all different within a row; in each aligned block of 32 rows (0 to 31, 32 to 63, ...) at most 32 rows name the same one
- route_weights: float32 [256, 4], replicated, may hold values from 0.1 to 0.6
- w_gate_up: bfloat16 [8, 2, 2880, 2880], P('dp', None, 'expert'), may hold values from -0.109375 to 0.109375
- w_down: bfloat16 [8, 2880, 2880], P('dp', 'expert'), may hold values from -0.15625 to 0.15625
Outputs:
- layer_out: bfloat16 [256, 2880], P('dp', 'expert')
Inputs may be any that keep to these rules, and one draw needn't show every extreme that they name: `expert_ids`: each row names 4 different experts; among any aligned block of 32 rows no expert is named by more than 32 rows.
All inputs are finite; a program needn't handle non-finite values.
Results may differ from a plain program's by a relative error of at most 0.018.
Values may be sent and summed in bfloat16 or wider, within the bound.
No kernel may reach another device: no remote copies, remote signals or barrier semaphores. Data moves between devices by JAX's collectives and lax.ppermute only.
A program may use at most 64 MiB of HBM per device.

v0:
```python
import math

import jax
import jax.numpy as jnp
from jax import lax
from jax.sharding import PartitionSpec as P

D = 2880
QUERY_HEADS = 32
KEY_VALUE_HEADS = 4
HEAD_SIZE = 64
WINDOW_LENGTH = 128
TOP = 4


norm_eps = 1e-05
swish_alpha = 1.702


def attend(queries, fresh_key, fresh_value, cached_keys, cached_values, lengths, sink_logit_rows):
    batch_count = queries.shape[0]
    head_groups = QUERY_HEADS // KEY_VALUE_HEADS
    query_head_rows = queries.reshape(batch_count, KEY_VALUE_HEADS, head_groups, HEAD_SIZE)
    key_rows = cached_keys.reshape(batch_count, WINDOW_LENGTH, KEY_VALUE_HEADS, HEAD_SIZE)
    value_rows = cached_values.reshape(batch_count, WINDOW_LENGTH, KEY_VALUE_HEADS, HEAD_SIZE)
    score_scale = 1.0 / math.sqrt(HEAD_SIZE)
    cache_scores = (
        jnp.einsum("bkgd,bwkd->bkgw", query_head_rows, key_rows, preferred_element_type=jnp.float32)
        * score_scale
    )
    own_scores = (
        jnp.einsum(
            "npwm,npm->npw",
            query_head_rows,
            fresh_key.reshape(batch_count, KEY_VALUE_HEADS, HEAD_SIZE),
            preferred_element_type=jnp.float32,
        )
        * score_scale
    )
    slots = jnp.arange(WINDOW_LENGTH, dtype=jnp.int32)
    valid = (slots[None, :] >= (WINDOW_LENGTH - lengths)[:, None])[:, None, None, :]
    sink_terms = sink_logit_rows.reshape(KEY_VALUE_HEADS, head_groups)[None]
    masked = jnp.where(valid, cache_scores, -jnp.inf)
    top = jnp.maximum(jnp.maximum(jnp.max(masked, axis=-1), own_scores), sink_terms)
    cache_exp = jnp.where(valid, jnp.exp(masked - top[..., None]), 0.0)
    self_exp = jnp.exp(own_scores - top)
    total = jnp.sum(cache_exp, axis=-1) + self_exp + jnp.exp(sink_terms - top)
    cache_prob = (cache_exp / total[..., None]).astype(jnp.bfloat16)
    own_probability = (self_exp / total).astype(jnp.bfloat16)
    blended = jnp.einsum(
        "bkgw,bwkd->bkgd", cache_prob, value_rows, preferred_element_type=jnp.float32
    )
    blended = blended + own_probability.astype(jnp.float32)[..., None] * fresh_value.reshape(
        batch_count, KEY_VALUE_HEADS, 1, HEAD_SIZE
    ).astype(jnp.float32)
    return blended.reshape(batch_count, QUERY_HEADS * HEAD_SIZE).astype(jnp.bfloat16)


def slot_onehot(named, capacity):
    counts = jnp.cumsum(named.astype(jnp.int32), axis=1) - 1
    places = jnp.arange(capacity, dtype=jnp.int32)
    return named[:, None, :] & (counts[:, None, :] == places[None, :, None])


def receiver_slots(expert_ids, route_weights, expert, blocks, capacity):
    picked = expert_ids == expert
    named = jnp.any(picked, axis=1).reshape(blocks, -1)
    weight_at = jnp.sum(jnp.where(picked, route_weights, 0.0), axis=1).reshape(blocks, -1)
    onehot = slot_onehot(named, capacity)
    slot_weight = jnp.sum(jnp.where(onehot, weight_at[:, None, :], 0.0), axis=2)
    return (onehot, slot_weight)


def sender_slots(my_ids, experts, capacity):
    labels = jnp.arange(experts, dtype=jnp.int32)
    named = jnp.any(my_ids[None, :, :] == labels[:, None, None], axis=2)
    return slot_onehot(named, capacity)


def body(
    queries,
    fresh_key,
    fresh_value,
    cached_keys,
    cached_values,
    lengths,
    sink_logit_rows,
    residual,
    o_weight,
    norm_gain,
    expert_ids,
    route_weights,
    w_gate_up,
    w_down,
):
    attended = attend(
        queries, fresh_key, fresh_value, cached_keys, cached_values, lengths, sink_logit_rows
    )
    projected = lax.dot_general(
        lax.all_gather(attended, "expert", axis=0, tiled=True),
        o_weight,
        (((1,), (1,)), ((), ())),
        preferred_element_type=jnp.float32,
    )
    stream = (residual.astype(jnp.float32) + projected).astype(jnp.bfloat16)
    wide = stream.astype(jnp.float32)
    group_rows = stream.shape[0]
    columns = stream.shape[1]
    experts = lax.axis_size("dp")
    capacity = 2 * group_rows * TOP // experts
    gain_cols = lax.dynamic_slice_in_dim(norm_gain, lax.axis_index("expert") * columns, columns)
    squares = lax.psum(jnp.sum(wide * wide, axis=1), "expert")
    score_scale = lax.rsqrt(squares / D + norm_eps)
    outgoing = (wide * score_scale[:, None] * gain_cols[None, :]).astype(jnp.bfloat16)
    onehot_in, slot_weight = receiver_slots(
        expert_ids, route_weights, lax.axis_index("dp"), experts, capacity
    )
    my_ids = lax.dynamic_slice_in_dim(expert_ids, lax.axis_index("dp") * group_rows, group_rows, 0)
    onehot_out = sender_slots(my_ids, experts, capacity)
    outbound = jnp.einsum(
        "ect,td->ecd", onehot_out.astype(jnp.bfloat16), outgoing, preferred_element_type=jnp.float32
    ).astype(jnp.bfloat16)
    received = lax.all_to_all(outbound, "dp", split_axis=0, concat_axis=0, tiled=True)
    rows = received.reshape(experts * capacity, columns)
    gate_up = w_gate_up[0]
    down = w_down[0]
    both = jnp.einsum(
        "rc,hfc->rhf",
        lax.all_gather(rows, "expert", axis=1, tiled=True),
        gate_up,
        preferred_element_type=jnp.float32,
    )
    gate = both[:, 0]
    up = both[:, 1]
    hidden = ((up + 1.0) * gate * jax.nn.sigmoid(swish_alpha * gate)).astype(jnp.bfloat16)
    summed = lax.psum_scatter(
        lax.dot_general(
            down, hidden, (((0,), (1,)), ((), ())), preferred_element_type=jnp.float32
        ).astype(jnp.bfloat16),
        "expert",
        scatter_dimension=0,
        tiled=True,
    ).astype(jnp.float32)
    contribution = (summed * slot_weight.reshape(1, -1)).astype(jnp.bfloat16)
    contribution = contribution.T.reshape(experts, capacity, columns)
    returned = lax.all_to_all(contribution, "dp", split_axis=0, concat_axis=0, tiled=True)
    returned_sum = jnp.einsum(
        "ect,ecd->td",
        onehot_out.astype(jnp.float32),
        returned.astype(jnp.float32),
        precision=lax.Precision.HIGHEST,
    )
    return (wide + returned_sum).astype(jnp.bfloat16)


def solution(mesh):
    placed = (
        P(("dp", "expert"), None),
        P(("dp", "expert"), None),
        P(("dp", "expert"), None),
        P(("dp", "expert"), None, None),
        P(("dp", "expert"), None, None),
        P(("dp", "expert")),
        P(),
        P("dp", "expert"),
        P("expert", None),
        P(),
        P(),
        P(),
        P("dp", None, "expert", None),
        P("dp", "expert", None),
    )
    return jax.shard_map(
        body, mesh=mesh, in_specs=placed, out_specs=P("dp", "expert"), check_vma=False
    )
```

profile of v0, /device:TPU:0, one launch (start us, length us, event | category | flops | bytes accessed | tf_op | source)
XLA Modules:
  0.0 138.2 jit_solution(12964307490870638373)
XLA Ops:
  6.5 0.0 copy-start
  6.5 0.0 all-gather.2.cloned.1.call-start
  6.5 0.8 broadcast_subtract_fusion
  7.4 0.1 iota_compare_fusion.3
  7.4 0.9 reshape.81
  8.4 1.3 copy.27
  9.7 1.4 reshape.94
  11.1 0.7 max.14
  11.8 0.9 fusion.48
  12.7 0.3 fusion.47
  13.0 0.2 fusion.28
  13.2 0.4 copy-done.1
  13.6 0.6 fusion.42
  14.3 1.3 copy.28
  15.6 0.0 copy-done.4
  15.6 0.7 reshape.87
  16.3 0.0 copy-done.3
  16.3 1.4 %fusion.12 = bf16[8,4,8,64]{3,2,1,0:T(8,128)(2,1)S(1)} fusion(bf16[8,128,4,64]{1,3,2,0:T(8,128)(2,1)S(1)} %bitcast.48, f32[8,4,8,128]{3,2,1,0:T(8,128)} %copy-done.1, f32[8,4,64]{2,1,0:T(4,128)} %reshape.87, f32[8,4,8]{2,1,0:T(4,128)} %get-tuple-element.7, f32[8,4,8]{2,1,0:T(4,128)} %get-tuple-element.8, f32[8,4,8]{2,1,0:T(4,128)S(1)} %maximum_maximum_fusion, ...), kind=kOutput, calls=%fused_computation.11 | convolution fusion | flops 4374528 | bytes 700416 | tf_op jit(solution)/shard_map/bkgw,bwkd->bkgd/dot_general | solution.py:50
  17.7 0.1 convert_element_type.86
  17.8 6.5 %all_gather.6 = bf16[32,2048]{1,0:T(8,128)(2,1)S(1)} all-gather(bf16[8,2048]{1,0:T(8,128)(2,1)S(1)} %convert_element_type.86), channel_id=1, replica_groups=mesh['dp'=8,'expert'=4] {'expert'}, dimensions={0}, use_global_device_ids=true | all-gather | bytes 163840 | tf_op jit(solution)/shard_map/all_gather | solution.py:100
  24.4 0.0 copy-done
  24.4 1.9 %multiply_reduce_fusion = (f32[32]{0:T(128)S(1)}, f32[32,720]{1,0:T(8,128)S(1)}) fusion(bf16[32,2048]{1,0:T(8,128)(2,1)S(1)} %all_gather.6, bf16[720,2048]{1,0:T(8,128)(2,1)S(1)} %copy-done, bf16[32,720]{1,0:T(8,128)(2,1)} %param.21), kind=kOutput, calls=%fused_computation.35 | convolution fusion | flops 94510048 | bytes 3218560 | tf_op jit(solution)/shard_map/dot_general | solution.py:99
  26.2 7.5 %psum.7 = f32[32]{0:T(128)S(1)} all-reduce(f32[32]{0:T(128)S(1)} %get-tuple-element.11), channel_id=1, replica_groups=mesh['dp'=8,'expert'=4] {'expert'}, use_global_device_ids=true, to_apply=%region_5.6 | all-reduce | flops 32 | bytes 256 | tf_op jit(solution)/shard_map/psum | solution.py:112
  33.7 0.8 constant_dynamic-slice_fusion
  34.5 0.2 reduce_window_sum.17
  34.7 0.8 dynamic_slice.7
  35.4 0.4 convolution_convert_fusion
  35.8 16.2 %all_to_all.10 = bf16[8,32,720]{2,1,0:T(8,128)(2,1)S(1)} all-to-all(bf16[8,32,720]{2,1,0:T(8,128)(2,1)S(1)} %convolution_convert_fusion), channel_id=1, replica_groups=mesh['dp'=8,'expert'=4] {'dp'}, dimensions={0} | all-to-all | bytes 737280 | tf_op jit(solution)/shard_map/all_to_all | solution.py:123
  52.1 0.9 copy.30
  53.0 0.0 all-gather.2.cloned.1.call-update
  53.0 0.0 reduce-scatter.2.cloned.1.call-start
  53.1 17.9 %all-gather.2.cloned.1.call-done = bf16[256,2880]{0,1:T(8,128)(2,1)} async-done(((bf16[256,720]{0,1:T(8,128)(2,1)}), bf16[256,2880]{0,1:T(8,128)(2,1)}) %all-gather.2.cloned.1.call-update) | async-done | bytes 1474576 | tf_op jit(solution)/shard_map/all_gather | solution.py:129
  71.0 6.3 %fusion = f32[256,2,720]{0,2,1:T(8,128)S(1)} fusion(bf16[1,2,720,2880]{3,2,1,0:T(8,128)(2,1)} %param.26, bf16[256,2880]{0,1:T(8,128)(2,1)} %all-gather.2.cloned.1.call-done), kind=kOutput, calls=%fused_computation | convolution fusion | flops 2123366400 | bytes 11243520 | tf_op jit(solution)/shard_map/rc,hfc->rhf/dot_general | solution.py:127
  77.3 0.0 copy-start.2
  77.3 0.0 copy-start.5
  77.3 5.3 %fusion.7 = bf16[2880,256]{1,0:T(8,128)(2,1)} fusion(bf16[1,720,2880]{2,1,0:T(8,128)(2,1)} %param.27, f32[256,2,720]{0,2,1:T(8,128)S(1)} %fusion), kind=kOutput, calls=%fused_computation.5 | convolution fusion | flops 1063895040 | bytes 7096320 | tf_op jit(solution)/shard_map/dot_general | solution.py:137
  82.6 0.0 reduce-scatter.2.cloned.1.call-update
  82.6 0.1 and.22
  82.7 0.2 reduce_window_sum.18
  82.9 0.0 copy-done.5
  83.0 0.1 broadcast_in_dim.55
  83.0 0.1 select_reduce_fusion
  83.2 0.1 mul.93
  83.2 27.0 %reduce-scatter.2.cloned.1.call-done = bf16[720,256]{1,0:T(8,128)(2,1)} async-done(((bf16[2880,256]{1,0:T(8,128)(2,1)}), bf16[720,256]{1,0:T(8,128)(2,1)}) %reduce-scatter.2.cloned.1.call-update) | async-done | bytes 368656 | tf_op jit(solution)/shard_map/reduce_scatter | solution.py:136
  110.2 1.8 %fusion.20 = bf16[256,720]{0,1:T(8,128)(2,1)} fusion(bf16[720,256]{1,0:T(8,128)(2,1)} %reduce-scatter.2.cloned.1.call-done, f32[256]{0:T(256)S(1)} %mul.93), kind=kLoop, calls=%fused_computation.23 | loop fusion | flops 552960 | bytes 738304 | tf_op jit(solution)/shard_map/transpose | solution.py:145
  112.0 1.2 copy.31
  113.2 17.2 %all_to_all.11 = bf16[8,32,720]{2,1,0:T(8,128)(2,1)S(1)} all-to-all(bf16[8,32,720]{2,1,0:T(8,128)(2,1)S(1)} %bitcast.47), channel_id=1, replica_groups=mesh['dp'=8,'expert'=4] {'dp'}, dimensions={0} | all-to-all | bytes 737280 | tf_op jit(solution)/shard_map/all_to_all | solution.py:146
  130.4 1.0 fusion.16
  (13 shorter events, 0.1 us)
Async XLA Ops:
  6.5 17.8 %copy-start = (bf16[720,2048]{1,0:T(8,128)(2,1)S(1)}, bf16[720,2048]{1,0:T(8,128)(2,1)}, u32[]{:S(2)}) copy-start(bf16[720,2048]{1,0:T(8,128)(2,1)} %param.22) | copy-start | bytes 8847364
  6.5 9.1 %copy-start.4 = (bf16[8,256]{1,0:T(8,128)(2,1)S(1)}, bf16[8,256]{1,0:T(8,128)(2,1)}, u32[]{:S(2)}) copy-start(bf16[8,256]{1,0:T(8,128)(2,1)} %param.16) | copy-start | bytes 12292
  6.5 64.4 %all-gather.2.cloned.1.call-start = ((), (), s32[]{:S(2)}) async-start(), calls=%async_computation.3 | async-start | bytes 1843200 | tf_op jit(solution)/shard_map/all_gather | solution.py:129
  7.4 8.9 %copy-start.3 = (pred[8,128]{1,0:T(8,128)(4,1)}, pred[8,128]{1,0:T(8,128)(4,1)S(1)}, u32[]{:S(2)}) copy-start(pred[8,128]{1,0:T(8,128)(4,1)S(1)} %iota_compare_fusion.3) | copy-start | bytes 3076
  13.0 0.6 copy-start.1
  53.0 57.2 %reduce-scatter.2.cloned.1.call-start = ((), (), s32[]{:S(2)}) async-start(), calls=%async_computation.4 | async-start | bytes 1843200 | tf_op jit(solution)/shard_map/reduce_scatter | solution.py:136
  77.3 5.3 %copy-start.2 = (s32[256,4]{0,1:T(4,128)S(1)}, s32[256,4]{0,1:T(4,128)}, u32[]{:S(2)}) copy-start(s32[256,4]{0,1:T(4,128)} %param.24) | copy-start | bytes 12292
  77.3 5.6 %copy-start.5 = (f32[256,4]{0,1:T(4,128)S(1)}, f32[256,4]{0,1:T(4,128)}, u32[]{:S(2)}) copy-start(f32[256,4]{0,1:T(4,128)} %param.25) | copy-start | bytes 12292
Sparse Core Ops, SparseCore 0:
  53.1 17.7 all-gather.1
  82.7 27.4 reduce-scatter.1
where the time goes:
time: 139 us; the launch traced here: 138 us
  blocking collectives  47.5 us (34%)
  waiting for transfers between devices  44.9 us (32%)
  matrix products  17.4 us (13%)
  between operations  13.5 us (10%)
  local copies, waits for them, and re-layouts  10.8 us (8%)
  other arithmetic  4.1 us (3%)
    reduce_scatter x1, waiting for transfers between devices, body(): lax.psum_scatter(lax.dot_general(down, hidden, (((0,), (1,)), ((), ())),...  27 us
    all_gather x1, waiting for transfers between devices, body(): lax.all_gather(rows, 'expert', axis=1, tiled=True)  17.9 us
    all_to_all x1, blocking collectives, body(): lax.all_to_all(contribution, 'dp', split_axis=0, concat_axis=0, tiled=True)  17.2 us
    all_to_all x1, blocking collectives, body(): lax.all_to_all(outbound, 'dp', split_axis=0, concat_axis=0, tiled=True)  16.2 us
    psum x1, blocking collectives, body(): squares = lax.psum(jnp.sum(wide * wide, axis=1), 'expert')  7.47 us
    all_gather x1, blocking collectives, body(): lax.all_gather(attended, 'expert', axis=0, tiled=True)  6.54 us
    dot_general x1, matrix products, body(): jnp.einsum('rc,hfc->rhf', lax.all_gather(rows, 'expert', axis=1, tiled=Tr...  6.32 us
    dot_general x1, matrix products, body(): lax.dot_general(down, hidden, (((0,), (1,)), ((), ())), preferred_element...  5.28 us
  transfers between devices with their start and end apart: 2, of which 2 were waited for; matrix products, arithmetic and copies ran while one was open for 0% of the time, Pallas kernels for 0%

commit v1 on v0

--- a/solution.py
+++ b/solution.py
@@ -1,8 +1,11 @@
+import functools
 import math
 
 import jax
 import jax.numpy as jnp
 from jax import lax
+from jax.experimental import pallas as pl
+from jax.experimental.pallas import tpu as pltpu
 from jax.sharding import PartitionSpec as P
 
 D = 2880
@@ -15,6 +18,246 @@
 
 norm_eps = 1e-05
 swish_alpha = 1.702
+MIB = 1 << 20
+
+
+def attend_kernel(
+    len_ref, sink_ref, q_hbm, fk_hbm, fv_hbm, ck_hbm, cv_hbm, o_hbm, gu_hbm,
+    out_ref, o_ref, gu_ref, q_ref, fk_ref, fv_ref, ck_ref, cv_ref, qs_ref, os_ref, sem
+):
+    ins = [(q_hbm, q_ref), (fk_hbm, fk_ref), (fv_hbm, fv_ref), (ck_hbm, ck_ref), (cv_hbm, cv_ref)]
+    ahead = [(o_hbm, o_ref), (gu_hbm, gu_ref)]
+    copies = [pltpu.make_async_copy(src, dst, sem.at[n]) for n, (src, dst) in enumerate(ins + ahead)]
+    for copy in copies:
+        copy.start()
+    batch, width = q_ref.shape
+    heads = sink_ref.shape[0]
+    size = width // heads
+    kv_heads = fk_ref.shape[1] // size
+    group = heads // kv_heads
+    window = ck_ref.shape[1]
+    scale = 1.0 / math.sqrt(size)
+    head_rows = lax.broadcasted_iota(jnp.int32, (heads, 1), 0)
+    sink = jnp.zeros((heads, 1), jnp.float32)
+    for h in range(heads):
+        sink = jnp.where(head_rows == h, sink_ref[h], sink)
+    qs_ref[...] = jnp.zeros(qs_ref.shape, jnp.float32)
+    slots = lax.broadcasted_iota(jnp.int32, (heads, window), 1)
+    copies[0].wait()
+    q = q_ref[...].astype(jnp.float32)
+    for h in range(heads):
+        k = h // group
+        qs_ref[:, h, k * size:(k + 1) * size] = q[:, h * size:(h + 1) * size]
+    for copy in copies[1:len(ins)]:
+        copy.wait()
+    fk = fk_ref[...].astype(jnp.float32)
+    fv = fv_ref[...].astype(jnp.float32)
+    for b in range(batch):
+        qb = qs_ref[b]
+        scores = lax.dot_general(
+            qb.astype(jnp.bfloat16), ck_ref[b], (((1,), (1,)), ((), ())), preferred_element_type=jnp.float32
+        ) * scale
+        own = jnp.sum(qb * fk[b:b + 1], axis=1, keepdims=True) * scale
+        scores = jnp.where(slots >= window - len_ref[b], scores, -jnp.inf)
+        top = jnp.maximum(jnp.maximum(jnp.max(scores, axis=1, keepdims=True), own), sink)
+        probs = jnp.exp(scores - top)
+        own = jnp.exp(own - top)
+        total = jnp.sum(probs, axis=1, keepdims=True) + own + jnp.exp(sink - top)
+        probs = (probs / total).astype(jnp.bfloat16)
+        own = (own / total).astype(jnp.bfloat16).astype(jnp.float32)
+        mixed = jnp.dot(probs, cv_ref[b], preferred_element_type=jnp.float32)
+        os_ref[b] = mixed + own * fv[b:b + 1]
+    for h in range(0, heads, 2):
+        k0 = h // group
+        k1 = (h + 1) // group
+        pair = jnp.concatenate(
+            [os_ref[:, h, k0 * size:(k0 + 1) * size], os_ref[:, h + 1, k1 * size:(k1 + 1) * size]], axis=1
+        )
+        out_ref[:, h * size:(h + 2) * size] = pair.astype(jnp.bfloat16)
+    for copy in copies[len(ins):]:
+        copy.wait()
+
+
+VMEM = pl.BlockSpec(memory_space=pltpu.VMEM)
+SMEM = pl.BlockSpec(memory_space=pltpu.SMEM)
+HBM = pl.BlockSpec(memory_space=pltpu.HBM)
+
+
+def attend_local(
+    queries, fresh_key, fresh_value, cached_keys, cached_values, lengths, sink_logit_rows, o_weight, w_gate_up
+):
+    ins = [queries, fresh_key, fresh_value, cached_keys, cached_values]
+    spread = (queries.shape[0], sink_logit_rows.shape[0], fresh_key.shape[1])
+    return pl.pallas_call(
+        attend_kernel,
+        out_shape=[jax.ShapeDtypeStruct(a.shape, jnp.bfloat16) for a in (queries, o_weight, w_gate_up)],
+        in_specs=[SMEM] * 2 + [HBM] * 7,
+        out_specs=[VMEM] * 3,
+        scratch_shapes=[pltpu.VMEM(a.shape, jnp.bfloat16) for a in ins] + [
+            pltpu.VMEM(spread, jnp.float32),
+            pltpu.VMEM(spread, jnp.float32),
+            pltpu.SemaphoreType.DMA((len(ins) + 2,)),
+        ],
+        compiler_params=pltpu.CompilerParams(vmem_limit_bytes=32 * MIB),
+        name="attend",
+    )(lengths, sink_logit_rows, *[pltpu.with_memory_space_constraint(a, pltpu.HBM) for a in ins + [o_weight, w_gate_up]])
+
+
+def project_kernel(*refs):
+    blocks, (w_ref, res_ref, out_ref, rows_ref) = refs[:-4], refs[-4:]
+    rows = blocks[0].shape[0]
+    place = lax.axis_index("expert")
+    for r, block in enumerate(blocks):
+        rows_ref[pl.ds(pl.multiple_of((place ^ r) * rows, rows), rows), :] = block[...].astype(jnp.float32)
+    projected = lax.dot_general(
+        rows_ref[...].astype(jnp.bfloat16), w_ref[...], (((1,), (1,)), ((), ())), preferred_element_type=jnp.float32
+    )
+    out_ref[...] = (res_ref[...].astype(jnp.float32) + projected).astype(jnp.bfloat16)
+
+
+def project(blocks, o_weight, residual):
+    rows, width = blocks[0].shape
+    return pl.pallas_call(
+        project_kernel,
+        out_shape=jax.ShapeDtypeStruct(residual.shape, jnp.bfloat16),
+        in_specs=[VMEM] * (len(blocks) + 1) + [pl.BlockSpec(residual.shape, lambda: (0, 0))],
+        out_specs=VMEM,
+        scratch_shapes=[pltpu.VMEM((rows * len(blocks), width), jnp.float32)],
+        compiler_params=pltpu.CompilerParams(vmem_limit_bytes=12 * MIB),
+        name="project",
+    )(*blocks, o_weight, residual)
+
+
+def expert_kernel(*refs, lo, ys):
+    halves = 2
+    pairs = lo * ys
+    near, far, keep, send = refs[:pairs], refs[pairs:2 * pairs], refs[2 * pairs + 5:3 * pairs + 5], refs[3 * pairs + 5:4 * pairs + 5]
+    gain_ref, ids_ref, route_ref, gu_ref, down_ref = refs[2 * pairs:2 * pairs + 5]
+    x_ref, weight_ref, down_buf, hidden_ref, sums_ref, sem = refs[4 * pairs + 5:]
+    span, columns = near[0].shape
+    width = x_ref.shape[1]
+    units = down_buf.shape[0]
+    members = ys * halves
+    step = units // 3 if units % 48 == 0 else units
+    group = lax.axis_index("dp")
+    place = lax.axis_index("expert")
+    copy = pltpu.make_async_copy(down_ref.at[0], down_buf, sem.at[0])
+    copy.start()
+
+    groups = weight_ref.shape[0]
+    tokens = ids_ref.shape[1]
+    rows = tokens // groups
+    zs = span // rows
+    weight = jnp.sum(jnp.where(ids_ref[...] == group, route_ref[...], 0.0), axis=0, keepdims=True)
+    weight = jnp.transpose(jnp.broadcast_to(weight, (8, tokens)))[:, :1]
+    for g in range(groups):
+        weight_ref[g] = weight[g * rows:(g + 1) * rows]
+
+    for x in range(lo):
+        squares = jnp.zeros((span, 1), jnp.float32)
+        for y in range(ys):
+            for blocks in (near, far):
+                v = blocks[x * ys + y][...].astype(jnp.float32)
+                squares = squares + jnp.sum(v * v, axis=1, keepdims=True)
+        scale = lax.rsqrt(squares / width + norm_eps)
+        for p in range(members):
+            @pl.when(place == p)
+            def _():
+                for r in range(members):
+                    j = p ^ r
+                    blocks = far if r % halves else near
+                    gain = gain_ref[:, j * columns:(j + 1) * columns]
+                    v = blocks[x * ys + r // halves][...].astype(jnp.float32)
+                    x_ref[x * span:(x + 1) * span, j * columns:(j + 1) * columns] = (v * scale * gain).astype(jnp.bfloat16)
+
+    x_all = x_ref[...]
+    contract = (((1,), (1,)), ((), ()))
+    for i in range(0, units, step):
+        gate = lax.dot_general(x_all, gu_ref[0, 0, i:i + step, :], contract, preferred_element_type=jnp.float32)
+        up = lax.dot_general(x_all, gu_ref[0, 1, i:i + step, :], contract, preferred_element_type=jnp.float32)
+        hidden_ref[:, i:i + step] = ((up + 1.0) * gate * jax.nn.sigmoid(swish_alpha * gate)).astype(jnp.bfloat16)
+    copy.wait()
+    hidden = hidden_ref[...]
+    for x in range(lo):
+        part = jnp.dot(hidden[x * span:(x + 1) * span], down_buf[...], preferred_element_type=jnp.float32)
+        scales = jnp.concatenate([weight_ref[group ^ (z * lo + x)] for z in range(zs)], axis=0)
+        sums_ref[...] = (part * scales).astype(jnp.bfloat16)
+        for p in range(members):
+            @pl.when(place == p)
+            def _():
+                for r in range(members):
+                    j = p ^ r
+                    blocks = send if r % halves else keep
+                    blocks[x * ys + r // halves][...] = sums_ref[:, j * columns:(j + 1) * columns]
+
+
+def expert_sums(near, far, norm_gain, expert_ids, route_weights, w_gate_up, w_down, groups, lo):
+    units, width = w_down.shape[1:]
+    pairs = len(near)
+    ys = pairs // lo
+    span, columns = near[0].shape
+    total = span * lo
+    outs = pl.pallas_call(
+        functools.partial(expert_kernel, lo=lo, ys=ys),
+        out_shape=[jax.ShapeDtypeStruct((span, columns), jnp.bfloat16)] * (2 * pairs),
+        in_specs=[VMEM] * (2 * pairs + 4) + [HBM],
+        out_specs=[VMEM] * (2 * pairs),
+        scratch_shapes=[
+            pltpu.VMEM((total, width), jnp.bfloat16),
+            pltpu.VMEM((groups, total // groups, 1), jnp.float32),
+            pltpu.VMEM((units, width), jnp.bfloat16),
+            pltpu.VMEM((total, units), jnp.bfloat16),
+            pltpu.VMEM((span, width), jnp.bfloat16),
+            pltpu.SemaphoreType.DMA((1,)),
+        ],
+        compiler_params=pltpu.CompilerParams(vmem_limit_bytes=36 * MIB),
+        name="experts",
+    )(
+        *near, *far, norm_gain[None, :], expert_ids.T, route_weights.T, w_gate_up,
+        pltpu.with_memory_space_constraint(w_down, pltpu.HBM)
+    )
+    return outs[:pairs], outs[pairs:]
+
+
+def dense_body(
+    queries, fresh_key, fresh_value, cached_keys, cached_values, lengths, sink_logit_rows, residual, o_weight,
+    norm_gain, expert_ids, route_weights, w_gate_up, w_down
+):
+    groups = lax.axis_size("dp")
+    members = lax.axis_size("expert")
+    lo, halves = 2, 2
+    zs, ys = groups // lo, members // halves
+    rows = residual.shape[0]
+
+    def swap(value, x=0, z=0, y=0, c=0):
+        flip = (z * lo + x) * members + y * halves + c
+        return lax.ppermute(value, ("dp", "expert"), [(i, i ^ flip) for i in range(groups * members)])
+
+    attended, o_weight, w_gate_up = attend_local(
+        queries, fresh_key, fresh_value, cached_keys, cached_values, lengths, sink_logit_rows, o_weight, w_gate_up
+    )
+    blocks = [attended] + [swap(attended, y=r // halves, c=r % halves) for r in range(1, members)]
+    stream = project(blocks, o_weight, residual)
+
+    others = [(x, y) for x in range(lo) for y in range(ys)][1:]
+    line = jnp.concatenate([stream] + [swap(stream, z=z) for z in range(1, zs)], axis=0)
+    near = [line] + [swap(line, x=x, y=y) for x, y in others]
+    far = [swap(block, c=1) for block in near]
+    keep, send = expert_sums(near, far, norm_gain, expert_ids, route_weights, w_gate_up, w_down, groups, lo)
+
+    def added(parts):
+        total = parts[0].astype(jnp.float32)
+        for part in parts[1:]:
+            total = total + part.astype(jnp.float32)
+        return total
+
+    def cut(value, i):
+        return value[i * rows:(i + 1) * rows]
+
+    chip = [added([own, swap(other, c=1)]).astype(jnp.bfloat16) for own, other in zip(keep, send)]
+    plane = added([chip[0]] + [swap(part, x=x, y=y) for part, (x, y) in zip(chip[1:], others)]).astype(jnp.bfloat16)
+    total = added([stream, cut(plane, 0)] + [swap(cut(plane, z), z=z) for z in range(1, zs)])
+    return total.astype(jnp.bfloat16)
 
 
 def attend(queries, fresh_key, fresh_value, cached_keys, cached_values, lengths, sink_logit_rows):
@@ -170,6 +413,14 @@
         P("dp", None, "expert", None),
         P("dp", "expert", None),
     )
+
+    def layer(*args):
+        group_rows = args[7].shape[0]
+        groups, members = mesh.shape["dp"], mesh.shape["expert"]
+        capacity = 2 * group_rows * TOP // groups
+        paired = groups & (groups - 1) == 0 and members & (members - 1) == 0 and groups > 1 and members > 1
+        return (dense_body if capacity >= group_rows and paired else body)(*args)
+
     return jax.shard_map(
-        body, mesh=mesh, in_specs=placed, out_specs=P("dp", "expert"), check_vma=False
-    )
+        layer, mesh=mesh, in_specs=placed, out_specs=P("dp", "expert"), check_vma=False
+    )

time: 139 us -> 64.4 us (0.46)
  blocking collectives: 47.5 us -> 0 us
  starting transfers between devices: 0.04 us -> 19.9 us
  matrix products: 17.4 us -> 0 us
  waiting for transfers between devices: 44.9 us -> 29.7 us
  between operations: 13.5 us -> 0.1 us
  Pallas kernels: 0 us -> 12.2 us
  local copies, waits for them, and re-layouts: 10.8 us -> 1.35 us
  other arithmetic: 4.1 us -> 0.99 us
    all_to_all x2 -> x0, blocking collectives: 33.5 us -> none  [the longest x1 17.2 us: body(): lax.all_to_all(contribution, 'dp', split_axis=0, concat_axis=0, tiled=True)]
    ppermute x0 -> x23, waiting for transfers between devices: none -> 29.7 us  [swap(): lax.ppermute(value, ('dp', 'expert'), [(i, i ^ flip) for i in range(group...]
    reduce_scatter x1 -> x0, waiting for transfers between devices: 27 us -> none  [body(): lax.psum_scatter(lax.dot_general(down, hidden, (((0,), (1,)), ((), ())),...]
    ppermute x0 -> x23, starting transfers between devices: none -> 19.9 us  [swap(): lax.ppermute(value, ('dp', 'expert'), [(i, i ^ flip) for i in range(group...]
    all_gather x1 -> x0, waiting for transfers between devices: 17.9 us -> none  [body(): lax.all_gather(rows, 'expert', axis=1, tiled=True)]
    dot_general x8 -> x0, matrix products: 17.4 us -> none  [the longest x1 6.32 us: body(): jnp.einsum('rc,hfc->rhf', lax.all_gather(rows, 'expert', axis=1, tiled=Tr...]
    pallas_call x0 -> x3, Pallas kernels: none -> 12.2 us  [the longest x1 6.04 us: expert_sums(): pl.pallas_call(functools.partial(expert_kernel, lo=lo, ys=ys), out_shape=...]
    psum x1 -> x0, blocking collectives: 7.47 us -> none  [body(): squares = lax.psum(jnp.sum(wide * wide, axis=1), 'expert')]
  transfers between devices with their start and end apart: 2 -> 23, of which waited for: 2 -> 16; matrix products, arithmetic and copies ran while one was open for 0% -> 0% of each run, Pallas kernels for 0% -> 0%
where the time goes in v1:
time: 64.4 us; the launch traced here: 64.2 us
  waiting for transfers between devices  29.7 us (46%)
  starting transfers between devices  19.9 us (31%)
  Pallas kernels  12.2 us (19%)
  local copies, waits for them, and re-layouts  1.35 us (2%)
  other arithmetic  0.99 us (2%)
    ppermute x23, waiting for transfers between devices, swap(): lax.ppermute(value, ('dp', 'expert'), [(i, i ^ flip) for i in range(group...  29.7 us
    ppermute x23, starting transfers between devices, swap(): lax.ppermute(value, ('dp', 'expert'), [(i, i ^ flip) for i in range(group...  19.9 us
    pallas_call x1, Pallas kernels, expert_sums(): pl.pallas_call(functools.partial(expert_kernel, lo=lo, ys=ys), out_shape=...  6.04 us
    pallas_call x1, Pallas kernels, attend_local(): pl.pallas_call(attend_kernel, out_shape=[jax.ShapeDtypeStruct(a.shape, jn...  5.28 us
    unnamed x12, local copies, waits for them, and re-layouts  1.33 us
  transfers between devices with their start and end apart: 23, of which 16 were waited for; matrix products, arithmetic and copies ran while one was open for 0% of the time, Pallas kernels for 0%

profile of v1, /device:TPU:0, one launch (start us, length us, event | category | flops | bytes accessed | tf_op | source)
XLA Modules:
  0.0 64.2 jit_solution(733964244150634993)
XLA Ops:
  0.0 0.7 %copy-done.3 = s32[8]{0:T(128)S(1)} copy-done((s32[8]{0:T(128)S(1)}, s32[8]{0:T(128)}, u32[]{:S(2)}) %copy-start.3) | copy-done | bytes 56
  0.7 0.7 %copy-done.4 = f32[32]{0:T(128)S(1)} copy-done((f32[32]{0:T(128)S(1)}, f32[32]{0:T(128)}, u32[]{:S(2)}) %copy-start.4) | copy-done | bytes 152
  1.3 5.3 %attend.1 = (bf16[8,2048]{1,0:T(8,128)(2,1)S(1)}, bf16[720,2048]{1,0:T(8,128)(2,1)S(1)}, bf16[1,2,720,2880]{3,2,1,0:T(8,128)(2,1)S(1)}) custom-call(s32[8]{0:T(128)S(1)} %copy-done.3, f32[32]{0:T(128)S(1)} %copy-done.4, bf16[8,2048]{1,0:T(8,128)(2,1)} %q_hbm.1, bf16[8,256]{1,0:T(8,128)(2,1)} %fk_hbm.1, bf16[8,256]{1,0:T(8,128)(2,1)} %fv_hbm.1, ...), custom_call_target="tpu_custom_call" | custom-call | tf_op jit(solution)/shard_map/attend/pallas_call | solution.py:91
  6.6 2.5 %collective-permute-start.2 = (bf16[8,2048]{1,0:T(8,128)(2,1)S(1)}, bf16[8,2048]{1,0:T(8,128)(2,1)S(1)}, u32[]{:S(2)}, u32[]{:S(2)}) collective-permute-start(bf16[8,2048]{1,0:T(8,128)(2,1)S(1)} %get-tuple-element.16.refs_0_), channel_id=1, source_target_pairs={{0,3},{1,2},{2,1},{3,0},{4,7},{5,6},{6,5},{7,4},{8,11},{9,10},{10,... | collective-permute-start | bytes 98312 | tf_op jit(solution)/shard_map/ppermute | solution.py:234
  9.1 0.6 collective-permute-start.1
  9.8 0.0 collective-permute-start
  9.8 1.1 %collective-permute-done.2.refs_3_ = bf16[8,2048]{1,0:T(8,128)(2,1)S(1)} collective-permute-done((bf16[8,2048]{1,0:T(8,128)(2,1)S(1)}, bf16[8,2048]{1,0:T(8,128)(2,1)S(1)}, u32[]{:S(2)}, u32[]{:S(2)}) %collective-permute-start.2) | collective-permute-done | bytes 32800 | tf_op jit(solution)/shard_map/ppermute | solution.py:234
  10.9 2.2 %collective-permute-done.1.refs_2_ = bf16[8,2048]{1,0:T(8,128)(2,1)S(1)} collective-permute-done((bf16[8,2048]{1,0:T(8,128)(2,1)S(1)}, bf16[8,2048]{1,0:T(8,128)(2,1)S(1)}, u32[]{:S(2)}, u32[]{:S(2)}) %collective-permute-start.1) | collective-permute-done | bytes 32800 | tf_op jit(solution)/shard_map/ppermute | solution.py:234
  13.1 0.9 %project.1 = bf16[32,720]{1,0:T(8,128)(2,1)S(1)} custom-call(bf16[8,2048]{1,0:T(8,128)(2,1)S(1)} %get-tuple-element.16.refs_0_, bf16[8,2048]{1,0:T(8,128)(2,1)S(1)} %collective-permute-done.refs_1_, bf16[8,2048]{1,0:T(8,128)(2,1)S(1)} %collective-permute-done.1.refs_2_, bf16[8,2048]{1,0:T(8,128)(2,1)S(1)} %collective-permute-done.2.refs_3_, ...), custom_call_target="tpu_custom_call" | custom-call | tf_op jit(solution)/shard_map/project/pallas_call | solution.py:120
  14.0 3.7 %collective-permute-start.5 = (bf16[32,720]{1,0:T(8,128)(2,1)S(1)}, bf16[32,720]{1,0:T(8,128)(2,1)S(1)}, u32[]{:S(2)}, u32[]{:S(2)}) collective-permute-start(bf16[32,720]{1,0:T(8,128)(2,1)S(1)} %project.1), channel_id=1, source_target_pairs={{0,24},{1,25},{2,26},{3,27},{4,28},{5,29},{6,30},{7,31},{8,16},{9,... | collective-permute-start | bytes 138248 | tf_op jit(solution)/shard_map/ppermute | solution.py:234
  17.7 0.8 %collective-permute-start.3 = (bf16[32,720]{1,0:T(8,128)(2,1)S(1)}, bf16[32,720]{1,0:T(8,128)(2,1)S(1)}, u32[]{:S(2)}, u32[]{:S(2)}) collective-permute-start(bf16[32,720]{1,0:T(8,128)(2,1)S(1)} %project.1), channel_id=1, source_target_pairs={{0,8},{1,9},{2,10},{3,11},{4,12},{5,13},{6,14},{7,15},{8,0},{9,1},... | collective-permute-start | bytes 138248 | tf_op jit(solution)/shard_map/ppermute | solution.py:234
  18.5 1.8 %collective-permute-done.5 = bf16[32,720]{1,0:T(8,128)(2,1)S(1)} collective-permute-done((bf16[32,720]{1,0:T(8,128)(2,1)S(1)}, bf16[32,720]{1,0:T(8,128)(2,1)S(1)}, u32[]{:S(2)}, u32[]{:S(2)}) %collective-permute-start.5) | collective-permute-done | bytes 46112 | tf_op jit(solution)/shard_map/ppermute | solution.py:234
  20.2 2.4 %collective-permute-done.4 = bf16[32,720]{1,0:T(8,128)(2,1)S(1)} collective-permute-done((bf16[32,720]{1,0:T(8,128)(2,1)S(1)}, bf16[32,720]{1,0:T(8,128)(2,1)S(1)}, u32[]{:S(2)}, u32[]{:S(2)}) %collective-permute-start.4) | collective-permute-done | bytes 46112 | tf_op jit(solution)/shard_map/ppermute | solution.py:234
  22.7 0.0 collective-permute-done.3
  22.7 2.0 %collective-permute-start.8 = (bf16[128,720]{1,0:T(8,128)(2,1)S(1)}, bf16[128,720]{1,0:T(8,128)(2,1)S(1)}, u32[]{:S(2)}, u32[]{:S(2)}) collective-permute-start(bf16[128,720]{1,0:T(8,128)(2,1)S(1)} %pad_maximum_fusion.refs_0_), channel_id=1, source_target_pairs={{0,6},{1,7},{2,4},{3,5},{4,2},{5,3},{6,0},{7,1},{8,14},{9,15},{10,... | collective-permute-start | bytes 552968 | tf_op jit(solution)/shard_map/ppermute | solution.py:234
  24.7 0.5 collective-permute-start.7
  25.2 1.0 %collective-permute-start.6 = (bf16[128,720]{1,0:T(8,128)(2,1)S(1)}, bf16[128,720]{1,0:T(8,128)(2,1)S(1)}, u32[]{:S(2)}, u32[]{:S(2)}) collective-permute-start(bf16[128,720]{1,0:T(8,128)(2,1)S(1)} %pad_maximum_fusion.refs_0_), channel_id=1, source_target_pairs={{0,2},{1,3},{2,0},{3,1},{4,6},{5,7},{6,4},{7,5},{8,10},{9,11},{10,... | collective-permute-start | bytes 552968 | tf_op jit(solution)/shard_map/ppermute | solution.py:234
  26.3 0.0 collective-permute-start.9
  26.3 5.2 %collective-permute-done.8.refs_3_ = bf16[128,720]{1,0:T(8,128)(2,1)S(1)} collective-permute-done((bf16[128,720]{1,0:T(8,128)(2,1)S(1)}, bf16[128,720]{1,0:T(8,128)(2,1)S(1)}, u32[]{:S(2)}, u32[]{:S(2)}) %collective-permute-start.8) | collective-permute-done | bytes 184352 | tf_op jit(solution)/shard_map/ppermute | solution.py:234
  31.4 0.0 collective-permute-start.12
  31.4 2.0 %collective-permute-done.7.refs_2_ = bf16[128,720]{1,0:T(8,128)(2,1)S(1)} collective-permute-done((bf16[128,720]{1,0:T(8,128)(2,1)S(1)}, bf16[128,720]{1,0:T(8,128)(2,1)S(1)}, u32[]{:S(2)}, u32[]{:S(2)}) %collective-permute-start.7) | collective-permute-done | bytes 184352 | tf_op jit(solution)/shard_map/ppermute | solution.py:234
  33.4 0.2 collective-permute-done.6.refs_1_
  33.6 0.3 collective-permute-start.10
  34.0 0.9 %collective-permute-done.11.refs_6_ = bf16[128,720]{1,0:T(8,128)(2,1)S(1)} collective-permute-done((bf16[128,720]{1,0:T(8,128)(2,1)S(1)}, bf16[128,720]{1,0:T(8,128)(2,1)S(1)}, u32[]{:S(2)}, u32[]{:S(2)}) %collective-permute-start.11) | collective-permute-done | bytes 184352 | tf_op jit(solution)/shard_map/ppermute | solution.py:234
  34.9 0.3 collective-permute-done.10.refs_5_
  35.2 6.0 %experts.1 = (bf16[128,720]{1,0:T(8,128)(2,1)S(1)}, bf16[128,720]{1,0:T(8,128)(2,1)S(1)}, bf16[128,720]{1,0:T(8,128)(2,1)S(1)}, bf16[128,720]{1,0:T(8,128)(2,1)S...) custom-call(bf16[128,720]{1,0:T(8,128)(2,1)S(1)} %pad_maximum_fusion, ...), custom_call_target="tpu_custom_call" | custom-call | tf_op jit(solution)/shard_map/experts/pallas_call | solution.py:200
  41.2 0.3 collective-permute-start.14
  41.5 0.3 collective-permute-start.13
  41.8 0.2 collective-permute-start.16
  42.0 0.3 collective-permute-start.18
  42.3 0.4 collective-permute-done.14
  42.7 0.1 add_convert_fusion.3
  42.8 1.2 %collective-permute-start.15 = (bf16[128,720]{1,0:T(8,128)(2,1)S(1)}, bf16[128,720]{1,0:T(8,128)(2,1)S(1)}, u32[]{:S(2)}, u32[]{:S(2)}) collective-permute-start(bf16[128,720]{1,0:T(8,128)(2,1)S(1)} %add_convert_fusion.3), channel_id=1, source_target_pairs={{0,2},{1,3},{2,0},{3,1},{4,6},{5,7},{6,4},{7,5},{8,10},{9,11},{10,... | collective-permute-start | bytes 552968 | tf_op jit(solution)/shard_map/ppermute | solution.py:234
  44.0 0.1 add_convert_fusion.2
  44.1 1.6 %collective-permute-start.17 = (bf16[128,720]{1,0:T(8,128)(2,1)S(1)}, bf16[128,720]{1,0:T(8,128)(2,1)S(1)}, u32[]{:S(2)}, u32[]{:S(2)}) collective-permute-start(bf16[128,720]{1,0:T(8,128)(2,1)S(1)} %add_convert_fusion.2), channel_id=1, source_target_pairs={{0,4},{1,5},{2,6},{3,7},{4,0},{5,1},{6,2},{7,3},{8,12},{9,13},{10,... | collective-permute-start | bytes 552968 | tf_op jit(solution)/shard_map/ppermute | solution.py:234
  45.6 0.1 add_convert_fusion.1
  45.7 0.9 %collective-permute-start.19 = (bf16[128,720]{1,0:T(8,128)(2,1)S(1)}, bf16[128,720]{1,0:T(8,128)(2,1)S(1)}, u32[]{:S(2)}, u32[]{:S(2)}) collective-permute-start(bf16[128,720]{1,0:T(8,128)(2,1)S(1)} %add_convert_fusion.1), channel_id=1, source_target_pairs={{0,6},{1,7},{2,4},{3,5},{4,2},{5,3},{6,0},{7,1},{8,14},{9,15},{10,... | collective-permute-start | bytes 552968 | tf_op jit(solution)/shard_map/ppermute | solution.py:234
  46.6 3.3 %collective-permute-done.15 = bf16[128,720]{1,0:T(8,128)(2,1)S(1)} collective-permute-done((bf16[128,720]{1,0:T(8,128)(2,1)S(1)}, bf16[128,720]{1,0:T(8,128)(2,1)S(1)}, u32[]{:S(2)}, u32[]{:S(2)}) %collective-permute-start.15) | collective-permute-done | bytes 184352 | tf_op jit(solution)/shard_map/ppermute | solution.py:234
  49.9 2.0 %collective-permute-done.17 = bf16[128,720]{1,0:T(8,128)(2,1)S(1)} collective-permute-done((bf16[128,720]{1,0:T(8,128)(2,1)S(1)}, bf16[128,720]{1,0:T(8,128)(2,1)S(1)}, u32[]{:S(2)}, u32[]{:S(2)}) %collective-permute-start.17) | collective-permute-done | bytes 184352 | tf_op jit(solution)/shard_map/ppermute | solution.py:234
  51.9 3.5 %collective-permute-done.19 = bf16[128,720]{1,0:T(8,128)(2,1)S(1)} collective-permute-done((bf16[128,720]{1,0:T(8,128)(2,1)S(1)}, bf16[128,720]{1,0:T(8,128)(2,1)S(1)}, u32[]{:S(2)}, u32[]{:S(2)}) %collective-permute-start.19) | collective-permute-done | bytes 184352 | tf_op jit(solution)/shard_map/ppermute | solution.py:234
  55.4 0.1 add_convert_fusion
  55.6 0.6 collective-permute-start.20
  56.2 2.4 %collective-permute-start.22 = (bf16[32,720]{1,0:T(8,128)(2,1)S(1)}, bf16[32,720]{1,0:T(8,128)(2,1)S(1)}, u32[]{:S(2)}, u32[]{:S(2)}) collective-permute-start(bf16[32,720]{1,0:T(8,128)(2,1)S(1)} %get-tuple-element.28), channel_id=1, source_target_pairs={{0,24},{1,25},{2,26},{3,27},{4,28},{5,29},{6,30},{7,31},{8,16},{9,... | collective-permute-start | bytes 138248 | tf_op jit(solution)/shard_map/ppermute | solution.py:234
  58.6 0.5 collective-permute-start.21
  59.1 1.1 %collective-permute-done.20 = bf16[32,720]{1,0:T(8,128)(2,1)S(1)} collective-permute-done((bf16[32,720]{1,0:T(8,128)(2,1)S(1)}, bf16[32,720]{1,0:T(8,128)(2,1)S(1)}, u32[]{:S(2)}, u32[]{:S(2)}) %collective-permute-start.20) | collective-permute-done | bytes 46112 | tf_op jit(solution)/shard_map/ppermute | solution.py:234
  60.3 1.9 %collective-permute-done.22 = bf16[32,720]{1,0:T(8,128)(2,1)S(1)} collective-permute-done((bf16[32,720]{1,0:T(8,128)(2,1)S(1)}, bf16[32,720]{1,0:T(8,128)(2,1)S(1)}, u32[]{:S(2)}, u32[]{:S(2)}) %collective-permute-start.22) | collective-permute-done | bytes 46112 | tf_op jit(solution)/shard_map/ppermute | solution.py:234
  62.2 1.4 %collective-permute-done.21 = bf16[32,720]{1,0:T(8,128)(2,1)S(1)} collective-permute-done((bf16[32,720]{1,0:T(8,128)(2,1)S(1)}, bf16[32,720]{1,0:T(8,128)(2,1)S(1)}, u32[]{:S(2)}, u32[]{:S(2)}) %collective-permute-start.21) | collective-permute-done | bytes 46112 | tf_op jit(solution)/shard_map/ppermute | solution.py:234
  63.6 0.7 %add_convert_fusion.5 = bf16[32,720]{1,0:T(8,128)(2,1)} fusion(bf16[32,720]{1,0:T(8,128)(2,1)S(1)} %collective-permute-done.22, bf16[32,720]{1,0:T(8,128)(2,1)S(1)} %collective-permute-done.21, bf16[32,720]{1,0:T(8,128)(2,1)S(1)} %collective-permute-done.20, bf16[32,720]{1,0:T(8,128)(2,1)S(1)} %project.1, bf16[128,720]{1,0:T(8,128)(2,1)S(1)} %add_convert_fusion), kind=kLoop, calls=%fused_computation.6 | loop fusion | flops 230400 | bytes 276480 | tf_op jit(solution)/shard_map/convert_element_type | solution.py:260
  (21 shorter events, 0.1 us)
Async XLA Ops:
  0.0 13.1 %copy-start = (bf16[32,720]{1,0:T(8,128)(2,1)S(1)}, bf16[32,720]{1,0:T(8,128)(2,1)}, u32[]{:S(2)}) copy-start(bf16[32,720]{1,0:T(8,128)(2,1)} %refs_5_.1) | copy-start | bytes 138244
  0.0 35.2 %copy-start.2 = (f32[256,4]{0,1:T(4,128)S(1)}, f32[256,4]{0,1:T(4,128)}, u32[]{:S(2)}) copy-start(f32[256,4]{0,1:T(4,128)} %param.25) | copy-start | bytes 12292
  0.0 0.7 %copy-start.3 = (s32[8]{0:T(128)S(1)}, s32[8]{0:T(128)}, u32[]{:S(2)}) copy-start(s32[8]{0:T(128)} %len_ref.1) | copy-start | bytes 100
  0.7 0.7 %copy-start.4 = (f32[32]{0:T(128)S(1)}, f32[32]{0:T(128)}, u32[]{:S(2)}) copy-start(f32[32]{0:T(128)} %sink_ref.1) | copy-start | bytes 388
  1.3 32.6 %copy-start.5 = (f32[2880]{0:T(1024)S(1)}, f32[2880]{0:T(1024)}, u32[]{:S(2)}) copy-start(f32[2880]{0:T(1024)} %param.23) | copy-start | bytes 34564
  1.3 33.8 %copy-start.1 = (s32[256,4]{0,1:T(4,128)S(1)}, s32[256,4]{0,1:T(4,128)}, u32[]{:S(2)}) copy-start(s32[256,4]{0,1:T(4,128)} %param.24) | copy-start | bytes 12292
  6.6 4.3 %collective-permute-start.2 = (bf16[8,2048]{1,0:T(8,128)(2,1)S(1)}, bf16[8,2048]{1,0:T(8,128)(2,1)S(1)}, u32[]{:S(2)}, u32[]{:S(2)}) collective-permute-start(bf16[8,2048]{1,0:T(8,128)(2,1)S(1)} %get-tuple-element.16.refs_0_), channel_id=1, source_target_pairs={{0,3},{1,2},{2,1},{3,0},{4,7},{5,6},{6,5},{7,4},{8,11},{9,10},{10,... | collective-permute-start | bytes 98312 | tf_op jit(solution)/shard_map/ppermute | solution.py:234
  9.1 4.0 %collective-permute-start.1 = (bf16[8,2048]{1,0:T(8,128)(2,1)S(1)}, bf16[8,2048]{1,0:T(8,128)(2,1)S(1)}, u32[]{:S(2)}, u32[]{:S(2)}) collective-permute-start(bf16[8,2048]{1,0:T(8,128)(2,1)S(1)} %get-tuple-element.16.refs_0_), channel_id=1, source_target_pairs={{0,2},{1,3},{2,0},{3,1},{4,6},{5,7},{6,4},{7,5},{8,10},{9,11},{10,... | collective-permute-start | bytes 98312 | tf_op jit(solution)/shard_map/ppermute | solution.py:234
  9.8 3.3 %collective-permute-start = (bf16[8,2048]{1,0:T(8,128)(2,1)S(1)}, bf16[8,2048]{1,0:T(8,128)(2,1)S(1)}, u32[]{:S(2)}, u32[]{:S(2)}) collective-permute-start(bf16[8,2048]{1,0:T(8,128)(2,1)S(1)} %get-tuple-element.16.refs_0_), channel_id=1, source_target_pairs={{0,1},{1,0},{2,3},{3,2},{4,5},{5,4},{6,7},{7,6},{8,9},{9,8},{10,11... | collective-permute-start | bytes 98312 | tf_op jit(solution)/shard_map/ppermute | solution.py:234
  14.0 6.2 %collective-permute-start.5 = (bf16[32,720]{1,0:T(8,128)(2,1)S(1)}, bf16[32,720]{1,0:T(8,128)(2,1)S(1)}, u32[]{:S(2)}, u32[]{:S(2)}) collective-permute-start(bf16[32,720]{1,0:T(8,128)(2,1)S(1)} %project.1), channel_id=1, source_target_pairs={{0,24},{1,25},{2,26},{3,27},{4,28},{5,29},{6,30},{7,31},{8,16},{9,... | collective-permute-start | bytes 138248 | tf_op jit(solution)/shard_map/ppermute | solution.py:234
  17.7 5.0 %collective-permute-start.4 = (bf16[32,720]{1,0:T(8,128)(2,1)S(1)}, bf16[32,720]{1,0:T(8,128)(2,1)S(1)}, u32[]{:S(2)}, u32[]{:S(2)}) collective-permute-start(bf16[32,720]{1,0:T(8,128)(2,1)S(1)} %project.1), channel_id=1, source_target_pairs={{0,16},{1,17},{2,18},{3,19},{4,20},{5,21},{6,22},{7,23},{8,24},{9,... | collective-permute-start | bytes 138248 | tf_op jit(solution)/shard_map/ppermute | solution.py:234
  17.7 5.0 %collective-permute-start.3 = (bf16[32,720]{1,0:T(8,128)(2,1)S(1)}, bf16[32,720]{1,0:T(8,128)(2,1)S(1)}, u32[]{:S(2)}, u32[]{:S(2)}) collective-permute-start(bf16[32,720]{1,0:T(8,128)(2,1)S(1)} %project.1), channel_id=1, source_target_pairs={{0,8},{1,9},{2,10},{3,11},{4,12},{5,13},{6,14},{7,15},{8,0},{9,1},... | collective-permute-start | bytes 138248 | tf_op jit(solution)/shard_map/ppermute | solution.py:234
  22.7 8.7 %collective-permute-start.8 = (bf16[128,720]{1,0:T(8,128)(2,1)S(1)}, bf16[128,720]{1,0:T(8,128)(2,1)S(1)}, u32[]{:S(2)}, u32[]{:S(2)}) collective-permute-start(bf16[128,720]{1,0:T(8,128)(2,1)S(1)} %pad_maximum_fusion.refs_0_), channel_id=1, source_target_pairs={{0,6},{1,7},{2,4},{3,5},{4,2},{5,3},{6,0},{7,1},{8,14},{9,15},{10,... | collective-permute-start | bytes 552968 | tf_op jit(solution)/shard_map/ppermute | solution.py:234
  24.7 8.8 %collective-permute-start.7 = (bf16[128,720]{1,0:T(8,128)(2,1)S(1)}, bf16[128,720]{1,0:T(8,128)(2,1)S(1)}, u32[]{:S(2)}, u32[]{:S(2)}) collective-permute-start(bf16[128,720]{1,0:T(8,128)(2,1)S(1)} %pad_maximum_fusion.refs_0_), channel_id=1, source_target_pairs={{0,4},{1,5},{2,6},{3,7},{4,0},{5,1},{6,2},{7,3},{8,12},{9,13},{10,... | collective-permute-start | bytes 552968 | tf_op jit(solution)/shard_map/ppermute | solution.py:234
  25.2 8.4 %collective-permute-start.6 = (bf16[128,720]{1,0:T(8,128)(2,1)S(1)}, bf16[128,720]{1,0:T(8,128)(2,1)S(1)}, u32[]{:S(2)}, u32[]{:S(2)}) collective-permute-start(bf16[128,720]{1,0:T(8,128)(2,1)S(1)} %pad_maximum_fusion.refs_0_), channel_id=1, source_target_pairs={{0,2},{1,3},{2,0},{3,1},{4,6},{5,7},{6,4},{7,5},{8,10},{9,11},{10,... | collective-permute-start | bytes 552968 | tf_op jit(solution)/shard_map/ppermute | solution.py:234
  26.3 7.7 %collective-permute-start.9 = (bf16[128,720]{1,0:T(8,128)(2,1)S(1)}, bf16[128,720]{1,0:T(8,128)(2,1)S(1)}, u32[]{:S(2)}, u32[]{:S(2)}) collective-permute-start(bf16[128,720]{1,0:T(8,128)(2,1)S(1)} %pad_maximum_fusion.refs_0_), channel_id=1, source_target_pairs={{0,1},{1,0},{2,3},{3,2},{4,5},{5,4},{6,7},{7,6},{8,9},{9,8},{10,11... | collective-permute-start | bytes 552968 | tf_op jit(solution)/shard_map/ppermute | solution.py:234
  31.4 2.5 %collective-permute-start.12 = (bf16[128,720]{1,0:T(8,128)(2,1)S(1)}, bf16[128,720]{1,0:T(8,128)(2,1)S(1)}, u32[]{:S(2)}, u32[]{:S(2)}) collective-permute-start(bf16[128,720]{1,0:T(8,128)(2,1)S(1)} %collective-permute-done.8.refs_3_), channel_id=1, source_target_pairs={{0,1},{1,0},{2,3},{3,2},{4,5},{5,4},{6,7},{7,6},{8,9},{9,8},{10,11... | collective-permute-start | bytes 552968 | tf_op jit(solution)/shard_map/ppermute | solution.py:234
  33.4 1.4 %collective-permute-start.11 = (bf16[128,720]{1,0:T(8,128)(2,1)S(1)}, bf16[128,720]{1,0:T(8,128)(2,1)S(1)}, u32[]{:S(2)}, u32[]{:S(2)}) collective-permute-start(bf16[128,720]{1,0:T(8,128)(2,1)S(1)} %collective-permute-done.7.refs_2_), channel_id=1, source_target_pairs={{0,1},{1,0},{2,3},{3,2},{4,5},{5,4},{6,7},{7,6},{8,9},{9,8},{10,11... | collective-permute-start | bytes 552968 | tf_op jit(solution)/shard_map/ppermute | solution.py:234
  33.6 1.6 %collective-permute-start.10 = (bf16[128,720]{1,0:T(8,128)(2,1)S(1)}, bf16[128,720]{1,0:T(8,128)(2,1)S(1)}, u32[]{:S(2)}, u32[]{:S(2)}) collective-permute-start(bf16[128,720]{1,0:T(8,128)(2,1)S(1)} %collective-permute-done.6.refs_1_), channel_id=1, source_target_pairs={{0,1},{1,0},{2,3},{3,2},{4,5},{5,4},{6,7},{7,6},{8,9},{9,8},{10,11... | collective-permute-start | bytes 552968 | tf_op jit(solution)/shard_map/ppermute | solution.py:234
  41.2 1.5 %collective-permute-start.14 = (bf16[128,720]{1,0:T(8,128)(2,1)S(1)}, bf16[128,720]{1,0:T(8,128)(2,1)S(1)}, u32[]{:S(2)}, u32[]{:S(2)}) collective-permute-start(bf16[128,720]{1,0:T(8,128)(2,1)S(1)} %get-tuple-element.22), channel_id=1, source_target_pairs={{0,1},{1,0},{2,3},{3,2},{4,5},{5,4},{6,7},{7,6},{8,9},{9,8},{10,11... | collective-permute-start | bytes 552968 | tf_op jit(solution)/shard_map/ppermute | solution.py:234
  41.5 5.1 %collective-permute-start.13 = (bf16[128,720]{1,0:T(8,128)(2,1)S(1)}, bf16[128,720]{1,0:T(8,128)(2,1)S(1)}, u32[]{:S(2)}, u32[]{:S(2)}) collective-permute-start(bf16[128,720]{1,0:T(8,128)(2,1)S(1)} %get-tuple-element.20), channel_id=1, source_target_pairs={{0,1},{1,0},{2,3},{3,2},{4,5},{5,4},{6,7},{7,6},{8,9},{9,8},{10,11... | collective-permute-start | bytes 552968 | tf_op jit(solution)/shard_map/ppermute | solution.py:234
  41.8 2.2 %collective-permute-start.16 = (bf16[128,720]{1,0:T(8,128)(2,1)S(1)}, bf16[128,720]{1,0:T(8,128)(2,1)S(1)}, u32[]{:S(2)}, u32[]{:S(2)}) collective-permute-start(bf16[128,720]{1,0:T(8,128)(2,1)S(1)} %get-tuple-element.24), channel_id=1, source_target_pairs={{0,1},{1,0},{2,3},{3,2},{4,5},{5,4},{6,7},{7,6},{8,9},{9,8},{10,11... | collective-permute-start | bytes 552968 | tf_op jit(solution)/shard_map/ppermute | solution.py:234
  42.0 3.6 %collective-permute-start.18 = (bf16[128,720]{1,0:T(8,128)(2,1)S(1)}, bf16[128,720]{1,0:T(8,128)(2,1)S(1)}, u32[]{:S(2)}, u32[]{:S(2)}) collective-permute-start(bf16[128,720]{1,0:T(8,128)(2,1)S(1)} %get-tuple-element.26), channel_id=1, source_target_pairs={{0,1},{1,0},{2,3},{3,2},{4,5},{5,4},{6,7},{7,6},{8,9},{9,8},{10,11... | collective-permute-start | bytes 552968 | tf_op jit(solution)/shard_map/ppermute | solution.py:234
  42.8 7.1 %collective-permute-start.15 = (bf16[128,720]{1,0:T(8,128)(2,1)S(1)}, bf16[128,720]{1,0:T(8,128)(2,1)S(1)}, u32[]{:S(2)}, u32[]{:S(2)}) collective-permute-start(bf16[128,720]{1,0:T(8,128)(2,1)S(1)} %add_convert_fusion.3), channel_id=1, source_target_pairs={{0,2},{1,3},{2,0},{3,1},{4,6},{5,7},{6,4},{7,5},{8,10},{9,11},{10,... | collective-permute-start | bytes 552968 | tf_op jit(solution)/shard_map/ppermute | solution.py:234
  44.1 7.8 %collective-permute-start.17 = (bf16[128,720]{1,0:T(8,128)(2,1)S(1)}, bf16[128,720]{1,0:T(8,128)(2,1)S(1)}, u32[]{:S(2)}, u32[]{:S(2)}) collective-permute-start(bf16[128,720]{1,0:T(8,128)(2,1)S(1)} %add_convert_fusion.2), channel_id=1, source_target_pairs={{0,4},{1,5},{2,6},{3,7},{4,0},{5,1},{6,2},{7,3},{8,12},{9,13},{10,... | collective-permute-start | bytes 552968 | tf_op jit(solution)/shard_map/ppermute | solution.py:234
  45.7 9.7 %collective-permute-start.19 = (bf16[128,720]{1,0:T(8,128)(2,1)S(1)}, bf16[128,720]{1,0:T(8,128)(2,1)S(1)}, u32[]{:S(2)}, u32[]{:S(2)}) collective-permute-start(bf16[128,720]{1,0:T(8,128)(2,1)S(1)} %add_convert_fusion.1), channel_id=1, source_target_pairs={{0,6},{1,7},{2,4},{3,5},{4,2},{5,3},{6,0},{7,1},{8,14},{9,15},{10,... | collective-permute-start | bytes 552968 | tf_op jit(solution)/shard_map/ppermute | solution.py:234
  55.6 4.7 %collective-permute-start.20 = (bf16[32,720]{1,0:T(8,128)(2,1)S(1)}, bf16[32,720]{1,0:T(8,128)(2,1)S(1)}, u32[]{:S(2)}, u32[]{:S(2)}) collective-permute-start(bf16[32,720]{1,0:T(8,128)(2,1)S(1)} %get-tuple-element.27), channel_id=1, source_target_pairs={{0,8},{1,9},{2,10},{3,11},{4,12},{5,13},{6,14},{7,15},{8,0},{9,1},... | collective-permute-start | bytes 138248 | tf_op jit(solution)/shard_map/ppermute | solution.py:234
  56.2 6.0 %collective-permute-start.22 = (bf16[32,720]{1,0:T(8,128)(2,1)S(1)}, bf16[32,720]{1,0:T(8,128)(2,1)S(1)}, u32[]{:S(2)}, u32[]{:S(2)}) collective-permute-start(bf16[32,720]{1,0:T(8,128)(2,1)S(1)} %get-tuple-element.28), channel_id=1, source_target_pairs={{0,24},{1,25},{2,26},{3,27},{4,28},{5,29},{6,30},{7,31},{8,16},{9,... | collective-permute-start | bytes 138248 | tf_op jit(solution)/shard_map/ppermute | solution.py:234
  58.6 5.0 %collective-permute-start.21 = (bf16[32,720]{1,0:T(8,128)(2,1)S(1)}, bf16[32,720]{1,0:T(8,128)(2,1)S(1)}, u32[]{:S(2)}, u32[]{:S(2)}) collective-permute-start(bf16[32,720]{1,0:T(8,128)(2,1)S(1)} %get-tuple-element.29), channel_id=1, source_target_pairs={{0,16},{1,17},{2,18},{3,19},{4,20},{5,21},{6,22},{7,23},{8,24},{9,... | collective-permute-start | bytes 138248 | tf_op jit(solution)/shard_map/ppermute | solution.py:234
